TPU v7x, 32 devices: a whole 2x2x4 slice. The times are simulated.
32 devices in a mesh: section: 8 (over z, core), expert: 4 (over y, x).
Axes of the slice: x: 2, y: 2, z: 4, core: 2. Of those that a mesh axis runs over, the one named last changes fastest.
Arguments:
- state: bfloat16 [8, 512, 2048], P('section', 'expert'), may hold values from -6 to 6
- norm_gain: float32 [8, 2048], P('section'), may hold values from 0.25 to 1.75
- expert_in: bfloat16 [8, 4, 2048, 1536], P('section', 'expert'), may hold values from -0.125 to 0.125
- expert_out: bfloat16 [8, 4, 768, 2048], P('section', 'expert'), may hold values from -0.21875 to 0.21875
- route_ids: int32 [3, 8, 512, 6], P(None, 'section', 'expert'), may hold values from 0 to 63, all different within a row
- route_weights: float32 [3, 8, 512, 6], P(None, 'section', 'expert'), may hold values from 0.3 to 3
Outputs:
- state_out: bfloat16 [8, 512, 2048], P('section', 'expert')
Inputs may be any that keep to these rules, and one draw needn't show every extreme that they name: `route_ids`: each token names 6 different experts.
All inputs are finite; a program needn't handle non-finite values.
Results may differ from a plain program's by a relative error of at most 0.02.
Values may be sent and summed in bfloat16 or wider, within the bound.
A program may use at most 64 MiB of HBM per device.

v0:
```python
import jax
import jax.numpy as jnp
from jax import lax
from jax.sharding import PartitionSpec as P

epsilon = 1e-06


def shifted(shard, axis, by):
    peers = lax.axis_size(axis)
    return lax.ppermute(shard, axis, [(i, (i + by) % peers) for i in range(peers)])


def normalize(hidden, gain_row):
    widened = hidden.astype(jnp.float32)
    rescale = lax.rsqrt(jnp.mean(widened * widened, axis=-1, keepdims=True) + epsilon)
    return (widened * rescale * gain_row).astype(jnp.bfloat16)


def slot_tables(chosen, experts, capacity):
    window = jnp.arange(experts, dtype=jnp.int32)
    choice_hits = (chosen[:, :, None] == window[None, None, :]).astype(jnp.int32)
    picked = jnp.sum(choice_hits, axis=1)
    rank_table = jnp.cumsum(picked, axis=0) - picked
    kept_table = picked * (rank_table < capacity).astype(jnp.int32)
    slot_index = jnp.arange(capacity, dtype=jnp.int32)
    slot_match = kept_table[:, :, None] * (
        rank_table[:, :, None] == slot_index[None, None, :]
    ).astype(jnp.int32)
    positions = jnp.arange(chosen.shape[0], dtype=jnp.int32)
    token_at = jnp.sum(slot_match * positions[:, None, None], axis=0)
    filled = jnp.sum(slot_match, axis=0)
    kept_hits = choice_hits * kept_table[:, None, :]
    kept_choice = jnp.sum(kept_hits, axis=2)
    flat_slot = jnp.sum(
        kept_hits * (window[None, None, :] * capacity + rank_table[:, None, :]), axis=2
    )
    return (token_at, filled, flat_slot, kept_choice)


def expert_forward(token_rows, inner_weight, outer_weight):
    projected = jnp.dot(token_rows, inner_weight, preferred_element_type=jnp.float32)
    hidden_units = outer_weight.shape[0]
    activated = (jax.nn.silu(projected[:, :hidden_units]) * projected[:, hidden_units:]).astype(
        jnp.bfloat16
    )
    return jnp.dot(activated, outer_weight, preferred_element_type=jnp.float32).astype(jnp.bfloat16)


def on_device(state, norm_gain, expert_in, expert_out, route_ids, route_weights):
    experts = lax.axis_size("expert")
    hidden = state[0]
    capacity = hidden.shape[0] // 4
    gain_row = norm_gain[0]
    inner_weight = expert_in[0, 0]
    outer_weight = expert_out[0, 0]
    for tick_index in range(route_ids.shape[0]):
        chosen = route_ids[tick_index, 0]
        weights = route_weights[tick_index, 0]
        carried = shifted(hidden, "section", 1)
        normed = normalize(hidden, gain_row)
        token_at, filled, flat_slot, kept_choice = slot_tables(chosen, experts, capacity)
        outbound = jnp.take(normed, token_at, axis=0) * filled[:, :, None].astype(jnp.bfloat16)
        arrived_rows = lax.all_to_all(outbound, "expert", split_axis=0, concat_axis=0, tiled=True)
        token_rows = arrived_rows.reshape(-1, arrived_rows.shape[-1])
        served = expert_forward(token_rows, inner_weight, outer_weight)
        returned = lax.all_to_all(
            served.reshape(arrived_rows.shape), "expert", split_axis=0, concat_axis=0, tiled=True
        )
        flat_rows = returned.reshape(-1, returned.shape[-1])
        picked_rows = jnp.take(flat_rows, flat_slot, axis=0)
        mixing = weights * kept_choice.astype(weights.dtype)
        branch = jnp.einsum("tk,tkd->td", mixing, picked_rows.astype(jnp.float32))
        arrived_branch = shifted(branch.astype(jnp.bfloat16), "section", 1).astype(branch.dtype)
        hidden = (carried.astype(jnp.float32) + arrived_branch).astype(jnp.bfloat16)
    return hidden[None]


def solution(mesh):
    in_specs = (
        P("section", "expert", None),
        P("section", None),
        P("section", "expert", None, None),
        P("section", "expert", None, None),
        P(None, "section", "expert", None),
        P(None, "section", "expert", None),
    )
    out_specs = P("section", "expert", None)
    return jax.shard_map(
        on_device, mesh=mesh, in_specs=in_specs, out_specs=out_specs, check_vma=False
    )
```

profile of v0, /device:TPU:0, one launch (start us, length us, event | category | flops | bytes accessed | tf_op | source)
XLA Modules:
  0.0 204.1 jit_solution(13138265522378929912)
XLA Ops:
  0.0 0.9 fusion.70
  1.0 0.2 reduce_window_sum.20
  1.3 0.2 select_reduce_fusion.2
  1.6 1.2 fusion.33
  3.0 2.0 %fusion.35 = bf16[128,2048]{1,0:T(8,128)(2,1)} fusion(f32[2048]{0:T(1024)} %bitcast.92, f32[128]{0:T(128)S(1)} %add_rsqrt_fusion.2, bf16[1,128,2048]{2,1,0:T(8,128)(2,1)} %param.10), kind=kLoop, calls=%fused_computation.41 | loop fusion | flops 1048576 | bytes 1057280 | tf_op jit(solution)/shard_map/convert_element_type | solution.py:17
  5.0 3.3 %gather_fusion = bf16[128,2048]{1,0:T(8,128)(2,1)} fusion(bf16[128,2048]{1,0:T(8,128)(2,1)} %fusion.35, s32[1024]{0:T(1024)S(1)} %pad_clamp_fusion.5), kind=kCustom, calls=%fused_computation.clone | custom fusion | bytes 1049088 | tf_op jit(solution)/shard_map/jit(_take)/gather | solution.py:63
  8.3 2.0 select_multiply_fusion.2
  10.3 5.2 %all-to-all-start = ((bf16[4,32,2048]{2,1,0:T(8,128)(2,1)}), bf16[4,32,2048]{2,1,0:T(8,128)(2,1)}, u32[]{:S(2)}, u32[]{:S(2)}) async-start(bf16[4,32,2048]{2,1,0:T(8,128)(2,1)} %select_multiply_fusion.2), calls=%async_computation | async-start | bytes 1048576 | tf_op jit(solution)/shard_map/all_to_all | solution.py:64
  15.5 0.6 iota_multiply_fusion
  16.1 0.6 fusion.71
  17.2 0.8 reduce_window_sum.25
  18.0 0.8 compare_select_fusion
  18.9 0.7 copy.30
  19.6 1.3 broadcast_add_fusion.2
  20.9 0.7 fusion.55
  21.6 0.7 fusion.63
  22.3 0.8 copy.43
  23.3 0.7 all-to-all-done
  24.1 4.0 %fusion.4 = f32[128,1536]{1,0:T(8,128)S(1)} fusion(bf16[128,2048]{1,0:T(8,128)(2,1)} %bitcast.5, bf16[1,1,2048,1536]{3,2,1,0:T(8,128)(2,1)} %param.12), kind=kOutput, calls=%fused_computation.10 | convolution fusion | flops 805306368 | bytes 7602176 | tf_op jit(solution)/shard_map/dot_general | solution.py:42
  28.1 1.4 fusion.21
  29.5 4.1 %all-to-all-start.1 = ((bf16[4,32,2048]{2,1,0:T(8,128)(2,1)}), bf16[4,32,2048]{2,1,0:T(8,128)(2,1)}, u32[]{:S(2)}, u32[]{:S(2)}) async-start(bf16[4,32,2048]{2,1,0:T(8,128)(2,1)} %bitcast.91), calls=%async_computation.1 | async-start | bytes 1048576 | tf_op jit(solution)/shard_map/all_to_all | solution.py:67
  33.8 0.2 select_reduce_fusion.1
  34.0 8.4 %all-to-all-done.1 = bf16[4,32,2048]{2,1,0:T(8,128)(2,1)} async-done(((bf16[4,32,2048]{2,1,0:T(8,128)(2,1)}), bf16[4,32,2048]{2,1,0:T(8,128)(2,1)}, u32[]{:S(2)}, u32[]{:S(2)}) %all-to-all-start.1) | async-done | bytes 524320 | tf_op jit(solution)/shard_map/all_to_all | solution.py:67
  42.4 8.2 %gather_fusion.1 = bf16[768,2048]{1,0:T(8,128)(2,1)} fusion(bf16[128,2048]{1,0:T(8,128)(2,1)} %bitcast.9, s32[1024]{0:T(1024)S(1)} %pad_clamp_fusion.4), kind=kCustom, calls=%fused_computation.1.clone | custom fusion | bytes 6294528 | tf_op jit(solution)/shard_map/jit(_take)/gather | solution.py:71
  50.7 6.3 %reshape.267 = bf16[128,6,2048]{2,1,0:T(8,128)(2,1)} reshape(bf16[768,2048]{1,0:T(8,128)(2,1)} %gather_fusion.1) | data formatting | bytes 6291456 | tf_op jit(solution)/shard_map/jit(_take)/gather | solution.py:71
  57.0 3.6 %fusion.10 = bf16[128,1,2048]{2,1,0:T(2,128)(2,1)S(1)} fusion(bf16[128,6,1]{1,2,0:T(2,128)(2,1)S(1)} %copy-done.5, bf16[128,6,2048]{2,1,0:T(8,128)(2,1)} %reshape.267, pred[128,6]{1,0:T(8,128)(4,1)S(1)} %copy.19), kind=kOutput, calls=%fused_computation.16 | convolution fusion | flops 4718592 | bytes 3672320 | tf_op jit(solution)/shard_map/tk,tkd->td/dot_general | solution.py:73
  60.5 1.1 copy.78
  61.6 0.5 collective-permute-start.1
  62.1 0.7 copy.40
  63.1 9.2 %collective-permute-done.1 = bf16[128,2048]{1,0:T(8,128)(2,1)} collective-permute-done((bf16[128,2048]{1,0:T(8,128)(2,1)}, bf16[128,2048]{1,0:T(8,128)(2,1)}, u32[]{:S(2)}, u32[]{:S(2)}) %collective-permute-start.1) | collective-permute-done | bytes 524320 | tf_op jit(solution)/shard_map/ppermute | solution.py:11
  72.3 1.5 fusion.36
  73.8 0.8 copy-done.1
  74.6 1.0 fusion.38
  75.6 3.3 %gather_fusion.2 = bf16[128,2048]{1,0:T(8,128)(2,1)} fusion(bf16[128,2048]{1,0:T(8,128)(2,1)} %fusion.38, s32[1024]{0:T(1024)S(1)} %pad_clamp_fusion.3), kind=kCustom, calls=%fused_computation.2.clone | custom fusion | bytes 1049088 | tf_op jit(solution)/shard_map/jit(_take)/gather | solution.py:63
  78.9 2.0 select_multiply_fusion.1
  80.9 4.1 %all-to-all-start.2 = ((bf16[4,32,2048]{2,1,0:T(8,128)(2,1)}), bf16[4,32,2048]{2,1,0:T(8,128)(2,1)}, u32[]{:S(2)}, u32[]{:S(2)}) async-start(bf16[4,32,2048]{2,1,0:T(8,128)(2,1)} %select_multiply_fusion.1), calls=%async_computation.2 | async-start | bytes 1048576 | tf_op jit(solution)/shard_map/all_to_all | solution.py:64
  85.4 6.2 %all-to-all-done.2 = bf16[4,32,2048]{2,1,0:T(8,128)(2,1)} async-done(((bf16[4,32,2048]{2,1,0:T(8,128)(2,1)}), bf16[4,32,2048]{2,1,0:T(8,128)(2,1)}, u32[]{:S(2)}, u32[]{:S(2)}) %all-to-all-start.2) | async-done | bytes 524320 | tf_op jit(solution)/shard_map/all_to_all | solution.py:64
  91.7 4.0 %fusion.2 = f32[128,1536]{1,0:T(8,128)S(1)} fusion(bf16[128,2048]{1,0:T(8,128)(2,1)} %bitcast.14, bf16[1,1,2048,1536]{3,2,1,0:T(8,128)(2,1)} %param.12), kind=kOutput, calls=%fused_computation.8 | convolution fusion | flops 805306368 | bytes 7602176 | tf_op jit(solution)/shard_map/dot_general | solution.py:42
  95.6 1.4 fusion.24
  97.1 4.3 %all-to-all-start.3 = ((bf16[4,32,2048]{2,1,0:T(8,128)(2,1)}), bf16[4,32,2048]{2,1,0:T(8,128)(2,1)}, u32[]{:S(2)}, u32[]{:S(2)}) async-start(bf16[4,32,2048]{2,1,0:T(8,128)(2,1)} %bitcast.90), calls=%async_computation.3 | async-start | bytes 1048576 | tf_op jit(solution)/shard_map/all_to_all | solution.py:67
  101.5 0.2 select_reduce_fusion
  101.8 6.2 %all-to-all-done.3 = bf16[4,32,2048]{2,1,0:T(8,128)(2,1)} async-done(((bf16[4,32,2048]{2,1,0:T(8,128)(2,1)}), bf16[4,32,2048]{2,1,0:T(8,128)(2,1)}, u32[]{:S(2)}, u32[]{:S(2)}) %all-to-all-start.3) | async-done | bytes 524320 | tf_op jit(solution)/shard_map/all_to_all | solution.py:67
  108.0 8.2 %gather_fusion.3 = bf16[768,2048]{1,0:T(8,128)(2,1)} fusion(bf16[128,2048]{1,0:T(8,128)(2,1)} %bitcast.16, s32[1024]{0:T(1024)S(1)} %pad_clamp_fusion.2), kind=kCustom, calls=%fused_computation.4.clone | custom fusion | bytes 6294528 | tf_op jit(solution)/shard_map/jit(_take)/gather | solution.py:71
  116.2 6.3 %reshape.275 = bf16[128,6,2048]{2,1,0:T(8,128)(2,1)} reshape(bf16[768,2048]{1,0:T(8,128)(2,1)} %gather_fusion.3) | data formatting | bytes 6291456 | tf_op jit(solution)/shard_map/jit(_take)/gather | solution.py:71
  122.5 3.5 %fusion.8 = bf16[128,1,2048]{2,1,0:T(2,128)(2,1)S(1)} fusion(bf16[128,6,1]{1,2,0:T(2,128)(2,1)S(1)} %copy.45, bf16[128,6,2048]{2,1,0:T(8,128)(2,1)} %reshape.275, pred[128,6]{1,0:T(8,128)(4,1)S(1)} %copy.29), kind=kOutput, calls=%fused_computation.14 | convolution fusion | flops 4718592 | bytes 3672320 | tf_op jit(solution)/shard_map/tk,tkd->td/dot_general | solution.py:73
  126.0 1.1 copy.77
  127.2 10.6 %collective-permute-done.3 = bf16[128,2048]{1,0:T(8,128)(2,1)} collective-permute-done((bf16[128,2048]{1,0:T(8,128)(2,1)}, bf16[128,2048]{1,0:T(8,128)(2,1)}, u32[]{:S(2)}, u32[]{:S(2)}) %collective-permute-start.3) | collective-permute-done | bytes 524320 | tf_op jit(solution)/shard_map/ppermute | solution.py:11
  137.8 1.5 fusion.39
  139.3 0.8 copy-done.2
  140.1 1.0 fusion.41
  141.1 3.3 %gather_fusion.4 = bf16[128,2048]{1,0:T(8,128)(2,1)} fusion(bf16[128,2048]{1,0:T(8,128)(2,1)} %fusion.41, s32[1024]{0:T(1024)S(1)} %pad_clamp_fusion.1), kind=kCustom, calls=%fused_computation.3.clone | custom fusion | bytes 1049088 | tf_op jit(solution)/shard_map/jit(_take)/gather | solution.py:63
  144.4 2.0 select_multiply_fusion
  146.4 4.1 %all-to-all-start.4 = ((bf16[4,32,2048]{2,1,0:T(8,128)(2,1)}), bf16[4,32,2048]{2,1,0:T(8,128)(2,1)}, u32[]{:S(2)}, u32[]{:S(2)}) async-start(bf16[4,32,2048]{2,1,0:T(8,128)(2,1)} %select_multiply_fusion), calls=%async_computation.4 | async-start | bytes 1048576 | tf_op jit(solution)/shard_map/all_to_all | solution.py:64
  150.7 6.5 %all-to-all-done.4 = bf16[4,32,2048]{2,1,0:T(8,128)(2,1)} async-done(((bf16[4,32,2048]{2,1,0:T(8,128)(2,1)}), bf16[4,32,2048]{2,1,0:T(8,128)(2,1)}, u32[]{:S(2)}, u32[]{:S(2)}) %all-to-all-start.4) | async-done | bytes 524320 | tf_op jit(solution)/shard_map/all_to_all | solution.py:64
  157.2 4.0 %fusion = f32[128,1536]{1,0:T(8,128)S(1)} fusion(bf16[128,2048]{1,0:T(8,128)(2,1)} %bitcast.21, bf16[1,1,2048,1536]{3,2,1,0:T(8,128)(2,1)} %param.12), kind=kOutput, calls=%fused_computation.6 | convolution fusion | flops 805306368 | bytes 7602176 | tf_op jit(solution)/shard_map/dot_general | solution.py:42
  161.1 1.4 fusion.27
  162.6 4.1 %all-to-all-start.5 = ((bf16[4,32,2048]{2,1,0:T(8,128)(2,1)}), bf16[4,32,2048]{2,1,0:T(8,128)(2,1)}, u32[]{:S(2)}, u32[]{:S(2)}) async-start(bf16[4,32,2048]{2,1,0:T(8,128)(2,1)} %bitcast.89), calls=%async_computation.5 | async-start | bytes 1048576 | tf_op jit(solution)/shard_map/all_to_all | solution.py:67
  167.3 6.0 %all-to-all-done.5 = bf16[4,32,2048]{2,1,0:T(8,128)(2,1)} async-done(((bf16[4,32,2048]{2,1,0:T(8,128)(2,1)}), bf16[4,32,2048]{2,1,0:T(8,128)(2,1)}, u32[]{:S(2)}, u32[]{:S(2)}) %all-to-all-start.5) | async-done | bytes 524320 | tf_op jit(solution)/shard_map/all_to_all | solution.py:67
  173.3 8.2 %gather_fusion.5 = bf16[768,2048]{1,0:T(8,128)(2,1)} fusion(bf16[128,2048]{1,0:T(8,128)(2,1)} %bitcast.23, s32[1024]{0:T(1024)S(1)} %pad_clamp_fusion), kind=kCustom, calls=%fused_computation.5.clone | custom fusion | bytes 6294528 | tf_op jit(solution)/shard_map/jit(_take)/gather | solution.py:71
  181.6 6.3 %reshape.283 = bf16[128,6,2048]{2,1,0:T(8,128)(2,1)} reshape(bf16[768,2048]{1,0:T(8,128)(2,1)} %gather_fusion.5) | data formatting | bytes 6291456 | tf_op jit(solution)/shard_map/jit(_take)/gather | solution.py:71
  187.8 3.5 %fusion.6 = bf16[128,1,2048]{2,1,0:T(2,128)(2,1)S(1)} fusion(bf16[128,6,1]{1,2,0:T(2,128)(2,1)S(1)} %copy.47, bf16[128,6,2048]{2,1,0:T(8,128)(2,1)} %reshape.283, pred[128,6]{1,0:T(8,128)(4,1)S(1)} %copy.39), kind=kOutput, calls=%fused_computation.12 | convolution fusion | flops 4718592 | bytes 3672320 | tf_op jit(solution)/shard_map/tk,tkd->td/dot_general | solution.py:73
  191.3 0.3 copy.76
  191.7 10.4 %collective-permute-done.5 = bf16[128,2048]{1,0:T(8,128)(2,1)S(1)} collective-permute-done((bf16[128,2048]{1,0:T(8,128)(2,1)S(1)}, bf16[128,2048]{1,0:T(8,128)(2,1)S(1)}, u32[]{:S(2)}, u32[]{:S(2)}) %collective-permute-start.5) | collective-permute-done | bytes 524320 | tf_op jit(solution)/shard_map/ppermute | solution.py:11
  202.1 2.0 fusion.42
  (90 shorter events, 3.2 us)
Async XLA Ops:
  0.0 28.0 %copy-start = (bf16[1,1,768,2048]{3,2,1,0:T(8,128)(2,1)S(1)}, bf16[1,1,768,2048]{3,2,1,0:T(8,128)(2,1)}, u32[]{:S(2)}) copy-start(bf16[1,1,768,2048]{3,2,1,0:T(8,128)(2,1)} %param.13) | copy-start | bytes 9437188
  1.3 9.1 %copy-start.6 = (s32[128,4]{0,1:T(4,128)}, s32[128,4]{0,1:T(4,128)S(1)}, u32[]{:S(2)}) copy-start(s32[128,4]{0,1:T(4,128)S(1)} %copy.17) | copy-start | bytes 6148
  1.6 14.5 %copy-start.9 = (f32[3,1,128,6]{2,1,3,0:T(1,128)S(1)}, f32[3,1,128,6]{2,1,3,0:T(1,128)}, u32[]{:S(2)}) copy-start(f32[3,1,128,6]{2,1,3,0:T(1,128)} %param.15) | copy-start | bytes 27652
  10.3 13.8 %all-to-all-start = ((bf16[4,32,2048]{2,1,0:T(8,128)(2,1)}), bf16[4,32,2048]{2,1,0:T(8,128)(2,1)}, u32[]{:S(2)}, u32[]{:S(2)}) async-start(bf16[4,32,2048]{2,1,0:T(8,128)(2,1)} %select_multiply_fusion.2), calls=%async_computation | async-start | bytes 1048576 | tf_op jit(solution)/shard_map/all_to_all | solution.py:64
  15.5 47.6 %collective-permute-start = (bf16[128,2048]{1,0:T(8,128)(2,1)}, bf16[128,2048]{1,0:T(8,128)(2,1)}, u32[]{:S(2)}, u32[]{:S(2)}) collective-permute-start(bf16[128,2048]{1,0:T(8,128)(2,1)} %bitcast.87), channel_id=1, source_target_pairs={{0,4},{4,8},{8,12},{12,16},{16,20},{20,24},{24,28},{28,0},{1,5},{5... | collective-permute-start | bytes 1572872 | tf_op jit(solution)/shard_map/ppermute | solution.py:11
  28.0 5.7 %copy-start.11 = (s32[128,4]{0,1:T(4,128)S(1)}, s32[128,4]{0,1:T(4,128)}, u32[]{:S(2)}) copy-start(s32[128,4]{0,1:T(4,128)} %copy.30) | copy-start | bytes 6148
  29.5 12.9 %all-to-all-start.1 = ((bf16[4,32,2048]{2,1,0:T(8,128)(2,1)}), bf16[4,32,2048]{2,1,0:T(8,128)(2,1)}, u32[]{:S(2)}, u32[]{:S(2)}) async-start(bf16[4,32,2048]{2,1,0:T(8,128)(2,1)} %bitcast.91), calls=%async_computation.1 | async-start | bytes 1048576 | tf_op jit(solution)/shard_map/all_to_all | solution.py:67
  50.7 6.3 %copy-start.5 = (bf16[128,6,1]{1,2,0:T(2,128)(2,1)S(1)}, bf16[128,6,1]{1,2,0:T(2,128)(2,1)}, u32[]{:S(2)}) copy-start(bf16[128,6,1]{1,2,0:T(2,128)(2,1)} %copy.43) | copy-start | bytes 4612
  56.9 5.9 %copy-start.3 = (s32[128,4]{1,0:T(8,128)S(1)}, s32[128,4]{1,0:T(8,128)}, u32[]{:S(2)}) copy-start(s32[128,4]{1,0:T(8,128)} %get-tuple-element.36) | copy-start | bytes 6148
  57.0 17.6 %copy-start.4 = (f32[1,2048]{1,0:T(1,128)S(1)}, f32[1,2048]{1,0:T(1,128)}, u32[]{:S(2)}) copy-start(f32[1,2048]{1,0:T(1,128)} %param.11) | copy-start | bytes 24580
  61.6 10.7 %collective-permute-start.1 = (bf16[128,2048]{1,0:T(8,128)(2,1)}, bf16[128,2048]{1,0:T(8,128)(2,1)}, u32[]{:S(2)}, u32[]{:S(2)}) collective-permute-start(bf16[128,2048]{1,0:T(8,128)(2,1)} %bitcast.82), channel_id=1, source_target_pairs={{0,4},{4,8},{8,12},{12,16},{16,20},{20,24},{24,28},{28,0},{1,5},{5... | collective-permute-start | bytes 1572872 | tf_op jit(solution)/shard_map/ppermute | solution.py:11
  73.8 0.8 copy-start.1
  73.8 11.2 %copy-start.8 = (f32[1,1,128,6]{2,1,3,0:T(1,128)S(1)}, f32[1,1,128,6]{2,1,3,0:T(1,128)}, u32[]{:S(2)}) copy-start(f32[1,1,128,6]{2,1,3,0:T(1,128)} %get-tuple-element.33) | copy-start | bytes 9220
  80.9 10.8 %all-to-all-start.2 = ((bf16[4,32,2048]{2,1,0:T(8,128)(2,1)}), bf16[4,32,2048]{2,1,0:T(8,128)(2,1)}, u32[]{:S(2)}, u32[]{:S(2)}) async-start(bf16[4,32,2048]{2,1,0:T(8,128)(2,1)} %select_multiply_fusion.1), calls=%async_computation.2 | async-start | bytes 1048576 | tf_op jit(solution)/shard_map/all_to_all | solution.py:64
  95.6 5.9 %copy-start.10 = (s32[128,4]{0,1:T(4,128)S(1)}, s32[128,4]{0,1:T(4,128)}, u32[]{:S(2)}) copy-start(s32[128,4]{0,1:T(4,128)} %copy.40) | copy-start | bytes 6148
  97.1 11.0 %all-to-all-start.3 = ((bf16[4,32,2048]{2,1,0:T(8,128)(2,1)}), bf16[4,32,2048]{2,1,0:T(8,128)(2,1)}, u32[]{:S(2)}, u32[]{:S(2)}) async-start(bf16[4,32,2048]{2,1,0:T(8,128)(2,1)} %bitcast.90), calls=%async_computation.3 | async-start | bytes 1048576 | tf_op jit(solution)/shard_map/all_to_all | solution.py:67
  101.8 25.5 %collective-permute-start.2 = (bf16[128,2048]{1,0:T(8,128)(2,1)}, bf16[128,2048]{1,0:T(8,128)(2,1)}, u32[]{:S(2)}, u32[]{:S(2)}) collective-permute-start(bf16[128,2048]{1,0:T(8,128)(2,1)} %copy-done.1), channel_id=1, source_target_pairs={{0,4},{4,8},{8,12},{12,16},{16,20},{20,24},{24,28},{28,0},{1,5},{5... | collective-permute-start | bytes 1572872 | tf_op jit(solution)/shard_map/ppermute | solution.py:11
  127.1 10.7 %collective-permute-start.3 = (bf16[128,2048]{1,0:T(8,128)(2,1)}, bf16[128,2048]{1,0:T(8,128)(2,1)}, u32[]{:S(2)}, u32[]{:S(2)}) collective-permute-start(bf16[128,2048]{1,0:T(8,128)(2,1)} %bitcast.81), channel_id=1, source_target_pairs={{0,4},{4,8},{8,12},{12,16},{16,20},{20,24},{24,28},{28,0},{1,5},{5... | collective-permute-start | bytes 1572872 | tf_op jit(solution)/shard_map/ppermute | solution.py:11
  139.3 0.8 copy-start.2
  139.3 11.3 %copy-start.7 = (f32[1,1,128,6]{2,1,3,0:T(1,128)S(1)}, f32[1,1,128,6]{2,1,3,0:T(1,128)}, u32[]{:S(2)}) copy-start(f32[1,1,128,6]{2,1,3,0:T(1,128)} %get-tuple-element.34) | copy-start | bytes 9220
  146.4 10.8 %all-to-all-start.4 = ((bf16[4,32,2048]{2,1,0:T(8,128)(2,1)}), bf16[4,32,2048]{2,1,0:T(8,128)(2,1)}, u32[]{:S(2)}, u32[]{:S(2)}) async-start(bf16[4,32,2048]{2,1,0:T(8,128)(2,1)} %select_multiply_fusion), calls=%async_computation.4 | async-start | bytes 1048576 | tf_op jit(solution)/shard_map/all_to_all | solution.py:64
  162.6 10.8 %all-to-all-start.5 = ((bf16[4,32,2048]{2,1,0:T(8,128)(2,1)}), bf16[4,32,2048]{2,1,0:T(8,128)(2,1)}, u32[]{:S(2)}, u32[]{:S(2)}) async-start(bf16[4,32,2048]{2,1,0:T(8,128)(2,1)} %bitcast.89), calls=%async_computation.5 | async-start | bytes 1048576 | tf_op jit(solution)/shard_map/all_to_all | solution.py:67
  167.3 24.5 %collective-permute-start.4 = (bf16[128,2048]{1,0:T(8,128)(2,1)}, bf16[128,2048]{1,0:T(8,128)(2,1)}, u32[]{:S(2)}, u32[]{:S(2)}) collective-permute-start(bf16[128,2048]{1,0:T(8,128)(2,1)} %copy-done.2), channel_id=1, source_target_pairs={{0,4},{4,8},{8,12},{12,16},{16,20},{20,24},{24,28},{28,0},{1,5},{5... | collective-permute-start | bytes 1572872 | tf_op jit(solution)/shard_map/ppermute | solution.py:11
  191.6 10.5 %collective-permute-start.5 = (bf16[128,2048]{1,0:T(8,128)(2,1)S(1)}, bf16[128,2048]{1,0:T(8,128)(2,1)S(1)}, u32[]{:S(2)}, u32[]{:S(2)}) collective-permute-start(bf16[128,2048]{1,0:T(8,128)(2,1)S(1)} %bitcast.88), channel_id=1, source_target_pairs={{0,4},{4,8},{8,12},{12,16},{16,20},{20,24},{24,28},{28,0},{1,5},{5... | collective-permute-start | bytes 1572872 | tf_op jit(solution)/shard_map/ppermute | solution.py:11
where the time goes:
time: 206 us; the launch traced here: 204 us
  waiting for transfers between devices  64.3 us (31%)
  local copies, waits for them, and re-layouts  63.6 us (31%)
  starting transfers between devices  26.7 us (13%)
  matrix products  26.7 us (13%)
  other arithmetic  22.3 us (11%)
    gather x6, local copies, waits for them, and re-layouts, on_device(): picked_rows = jnp.take(flat_rows, flat_slot, axis=0)  43.5 us
    ppermute x6, waiting for transfers between devices, shifted(): lax.ppermute(shard, axis, [(i, (i + by) % peers) for i in range(peers)])  30.2 us
    all_to_all x3, waiting for transfers between devices, on_device(): lax.all_to_all(served.reshape(arrived_rows.shape), 'expert', split_axis=0...  20.6 us
    all_to_all x3, starting transfers between devices, on_device(): lax.all_to_all(outbound, 'expert', split_axis=0, concat_axis=0, tiled=True)  13.4 us
    all_to_all x3, waiting for transfers between devices, on_device(): lax.all_to_all(outbound, 'expert', split_axis=0, concat_axis=0, tiled=True)  13.4 us
    all_to_all x3, starting transfers between devices, on_device(): lax.all_to_all(served.reshape(arrived_rows.shape), 'expert', split_axis=0...  12.6 us
    dot_general x3, matrix products, expert_forward(): jnp.dot(token_rows, inner_weight, preferred_element_type=jnp.float32)  11.9 us
    dot_general x3, matrix products, on_device(): branch = jnp.einsum('tk,tkd->td', mixing, picked_rows.astype(jnp.float32))  10.6 us
  transfers between devices with their start and end apart: 12, of which 9 were waited for; matrix products, arithmetic and copies ran while one was open for 36% of the time, Pallas kernels for 0%

commit v1 on v0

v1 whole, which is shorter than its diff:
```python
import functools

import jax
import jax.numpy as jnp
from jax import lax
from jax.experimental import pallas as pl
from jax.experimental.pallas import tpu as pltpu
from jax.sharding import PartitionSpec as P

epsilon = 1e-06
CHUNKS = 4
MESH = pl.DeviceIdType.MESH


def relay_kernel(
    sections,
    experts,
    state_ref,
    gain_ref,
    win_hbm,
    wout_hbm,
    ids_ref,
    wts_ref,
    out_ref,
    win,
    wout,
    hcur,
    hrecv,
    gather,
    comb_send,
    comb_recv,
    sendbuf,
    recvbuf,
    acc,
    retsend,
    retrecv,
    win_sem,
    wout_sem,
    disp_ss,
    disp_rs,
    ret_ss,
    ret_rs,
    h_ss,
    h_rs,
    comb_ss,
    comb_rs,
):
    ticks = ids_ref.shape[0]
    top = ids_ref.shape[3]
    tokens = state_ref.shape[1]
    width = state_ref.shape[2]
    chunks = win.shape[0]
    cols = width // chunks
    hidden_units = wout.shape[0]
    capacity = tokens // 4
    slots = experts * capacity

    section = lax.axis_index("section")
    me = lax.axis_index("expert")
    after = lax.rem(section + 1, sections)
    before = lax.rem(section + sections - 1, sections)

    barrier = pltpu.get_barrier_semaphore()
    for d in range(1, experts):
        peer = lax.rem(me + d, experts)
        pl.semaphore_signal(
            barrier, inc=1, device_id={"section": section, "expert": peer}, device_id_type=MESH
        )
    for e in range(experts):
        for other in (after, before):
            pl.semaphore_signal(
                barrier, inc=1, device_id={"section": other, "expert": e}, device_id_type=MESH
            )

    def load_in(c):
        return pltpu.make_async_copy(
            win_hbm.at[0, 0, pl.ds(c * cols, cols)], win.at[c], win_sem.at[c]
        )

    load_out = pltpu.make_async_copy(wout_hbm.at[0, 0], wout, wout_sem)
    for c in range(chunks):
        load_in(c).start()
    load_out.start()

    lane = lax.broadcasted_iota(jnp.int32, (tokens, slots), 1)
    expert_of = jnp.zeros((tokens, slots), jnp.int32)
    for e in range(1, experts):
        expert_of = expert_of + (lane >= e * capacity).astype(jnp.int32)
    slot_of = (lane - expert_of * capacity).astype(jnp.float32)
    row_i = lax.broadcasted_iota(jnp.int32, (tokens, tokens), 0)
    col_i = lax.broadcasted_iota(jnp.int32, (tokens, tokens), 1)
    earlier = jnp.where(col_i < row_i, 1.0, 0.0).astype(jnp.bfloat16)

    def tables(t):
        ids = ids_ref[t, 0]
        wts = wts_ref[t, 0]
        hit = jnp.zeros((tokens, slots), jnp.float32)
        mix = jnp.zeros((tokens, slots), jnp.float32)
        for k in range(top):
            match = ids[:, k : k + 1] == expert_of
            hit = jnp.where(match, 1.0, hit)
            mix = jnp.where(match, wts[:, k : k + 1], mix)
        rank = jnp.dot(earlier, hit.astype(jnp.bfloat16), preferred_element_type=jnp.float32)
        keep = jnp.where(rank == slot_of, hit, 0.0)
        gather[t] = jnp.transpose(keep).astype(jnp.bfloat16)
        comb_send[t] = (keep * mix).astype(jnp.bfloat16)

    def comb_copy(t):
        return pltpu.make_async_remote_copy(
            src_ref=comb_send.at[t],
            dst_ref=comb_recv.at[t],
            send_sem=comb_ss.at[t],
            recv_sem=comb_rs.at[t],
            device_id={"section": after, "expert": me},
            device_id_type=MESH,
        )

    def h_copy(t, c):
        source = state_ref.at[0, :, pl.ds(c * cols, cols)] if t == 0 else hcur.at[t - 1, c]
        return pltpu.make_async_remote_copy(
            src_ref=source,
            dst_ref=hrecv.at[t, c],
            send_sem=h_ss.at[t, c],
            recv_sem=h_rs.at[t, c],
            device_id={"section": after, "expert": me},
            device_id_type=MESH,
        )

    def disp_copy(t, c, d):
        peer = lax.rem(me + d, experts)
        return pltpu.make_async_remote_copy(
            src_ref=sendbuf.at[t, c, pl.ds(peer * capacity, capacity)],
            dst_ref=recvbuf.at[t, c, pl.ds(me * capacity, capacity)],
            send_sem=disp_ss.at[t, c, d - 1],
            recv_sem=disp_rs.at[t, c, d - 1],
            device_id={"section": section, "expert": peer},
            device_id_type=MESH,
        )

    def disp_arrival(t, c, d):
        source = lax.rem(me + experts - d, experts)
        block = recvbuf.at[t, c, pl.ds(source * capacity, capacity)]
        return pltpu.make_async_remote_copy(
            src_ref=block,
            dst_ref=block,
            send_sem=disp_ss.at[t, c, d - 1],
            recv_sem=disp_rs.at[t, c, d - 1],
            device_id={"section": section, "expert": source},
            device_id_type=MESH,
        )

    def ret_copy(t, c, d):
        peer = lax.rem(me + d, experts)
        return pltpu.make_async_remote_copy(
            src_ref=retsend.at[t, c, pl.ds(peer * capacity, capacity)],
            dst_ref=retrecv.at[t, c, pl.ds(me * capacity, capacity)],
            send_sem=ret_ss.at[t, c, d],
            recv_sem=ret_rs.at[t, c, d],
            device_id={"section": after, "expert": peer},
            device_id_type=MESH,
        )

    def ret_arrival(t, c, d):
        source = lax.rem(me + experts - d, experts)
        block = retrecv.at[t, c, pl.ds(source * capacity, capacity)]
        return pltpu.make_async_remote_copy(
            src_ref=block,
            dst_ref=block,
            send_sem=ret_ss.at[t, c, d],
            recv_sem=ret_rs.at[t, c, d],
            device_id={"section": before, "expert": source},
            device_id_type=MESH,
        )

    def fill(t, c, chunk):
        rows = jnp.dot(gather[t], chunk, preferred_element_type=jnp.float32)
        sendbuf[t, c] = rows.astype(jnp.bfloat16)

    def keep_own(t, c):
        own = pl.ds(pl.multiple_of(me * capacity, capacity), capacity)
        recvbuf[t, c, own, :] = sendbuf[t, c, own, :]

    tables(0)
    fill(0, 0, state_ref[0, :, pl.ds(0, cols)])
    pl.semaphore_wait(barrier, experts - 1 + 2 * experts)
    for c in range(chunks):
        if c:
            fill(0, c, state_ref[0, :, pl.ds(c * cols, cols)])
        for d in range(1, experts):
            disp_copy(0, c, d).start()
        keep_own(0, c)
    comb_copy(0).start()
    for c in range(chunks):
        h_copy(0, c).start()
    for t in range(1, ticks):
        tables(t)
        comb_copy(t).start()

    for t in range(ticks):
        squares = jnp.zeros((slots, 1), jnp.float32)
        for c in range(chunks):
            if t == 0:
                load_in(c).wait()
            for d in range(1, experts):
                disp_arrival(t, c, d).wait_recv()
            wide = recvbuf[t, c].astype(jnp.float32)
            squares = squares + jnp.sum(wide * wide, axis=-1, keepdims=True)
            scaled = (wide * gain_ref[:, pl.ds(c * cols, cols)]).astype(jnp.bfloat16)
            part = jnp.dot(scaled, win[c], preferred_element_type=jnp.float32)
            if c == 0:
                acc[...] = part
            else:
                acc[...] += part
        rescale = lax.rsqrt(squares / width + epsilon)
        gate = acc[:, :hidden_units] * rescale
        up = acc[:, hidden_units:] * rescale
        activated = (gate / (1.0 + jnp.exp(-gate)) * up).astype(jnp.bfloat16)
        if t == 0:
            load_out.wait()
        for c in range(chunks):
            served = jnp.dot(
                activated, wout[:, pl.ds(c * cols, cols)], preferred_element_type=jnp.float32
            )
            retsend[t, c] = served.astype(jnp.bfloat16)
            for d in range(experts):
                ret_copy(t, c, d).start()
        for c in range(chunks):
            if c == 0:
                comb_copy(t).wait_recv()
            h_copy(t, c).wait_recv()
            for d in range(experts):
                ret_arrival(t, c, d).wait_recv()
            branch = jnp.dot(comb_recv[t], retrecv[t, c], preferred_element_type=jnp.float32)
            fresh = (hrecv[t, c].astype(jnp.float32) + branch).astype(jnp.bfloat16)
            if t == ticks - 1:
                out_ref[0, :, pl.ds(c * cols, cols)] = fresh
            else:
                hcur[t, c] = fresh
                fill(t + 1, c, fresh)
                for d in range(1, experts):
                    disp_copy(t + 1, c, d).start()
                h_copy(t + 1, c).start()
                keep_own(t + 1, c)

    for t in range(ticks):
        comb_copy(t).wait_send()
        for c in range(chunks):
            h_copy(t, c).wait_send()
            for d in range(experts):
                if d:
                    disp_copy(t, c, d).wait_send()
                ret_copy(t, c, d).wait_send()


def on_device(sections, experts, state, norm_gain, expert_in, expert_out, route_ids, route_weights):
    ticks = route_ids.shape[0]
    tokens, width = state.shape[1:]
    inner = expert_in.shape[3]
    hidden_units = expert_out.shape[2]
    slots = experts * (tokens // 4)
    cols = width // CHUNKS
    bf16 = jnp.bfloat16
    vmem = pl.BlockSpec(memory_space=pltpu.VMEM)
    hbm = pl.BlockSpec(memory_space=pl.ANY)
    dma = pltpu.SemaphoreType.DMA
    return pl.pallas_call(
        functools.partial(relay_kernel, sections, experts),
        out_shape=jax.ShapeDtypeStruct(state.shape, state.dtype),
        in_specs=[vmem, vmem, hbm, hbm, vmem, vmem],
        out_specs=vmem,
        scratch_shapes=[
            pltpu.VMEM((CHUNKS, cols, inner), bf16),
            pltpu.VMEM((hidden_units, width), bf16),
            pltpu.VMEM((max(ticks - 1, 1), CHUNKS, tokens, cols), bf16),
            pltpu.VMEM((ticks, CHUNKS, tokens, cols), bf16),
            pltpu.VMEM((ticks, slots, tokens), bf16),
            pltpu.VMEM((ticks, tokens, slots), bf16),
            pltpu.VMEM((ticks, tokens, slots), bf16),
            pltpu.VMEM((ticks, CHUNKS, slots, cols), bf16),
            pltpu.VMEM((ticks, CHUNKS, slots, cols), bf16),
            pltpu.VMEM((slots, inner), jnp.float32),
            pltpu.VMEM((ticks, CHUNKS, slots, cols), bf16),
            pltpu.VMEM((ticks, CHUNKS, slots, cols), bf16),
            dma((CHUNKS,)),
            dma,
            dma((ticks, CHUNKS, experts - 1)),
            dma((ticks, CHUNKS, experts - 1)),
            dma((ticks, CHUNKS, experts)),
            dma((ticks, CHUNKS, experts)),
            dma((ticks, CHUNKS)),
            dma((ticks, CHUNKS)),
            dma((ticks,)),
            dma((ticks,)),
        ],
        compiler_params=pltpu.CompilerParams(
            collective_id=0, has_side_effects=True, vmem_limit_bytes=60 * 1024 * 1024
        ),
        name="relay",
    )(state, norm_gain, expert_in, expert_out, route_ids, route_weights)


def solution(mesh):
    in_specs = (
        P("section", "expert", None),
        P("section", None),
        P("section", "expert", None, None),
        P("section", "expert", None, None),
        P(None, "section", "expert", None),
        P(None, "section", "expert", None),
    )
    out_specs = P("section", "expert", None)
    return jax.shard_map(
        functools.partial(on_device, mesh.shape["section"], mesh.shape["expert"]),
        mesh=mesh,
        in_specs=in_specs,
        out_specs=out_specs,
        check_vma=False,
    )
```

time: 206 us -> 60.4 us (0.29)
  waiting for transfers between devices: 64.3 us -> 0 us
  local copies, waits for them, and re-layouts: 63.6 us -> 4.91 us
  Pallas kernels: 0 us -> 55.2 us
  matrix products: 26.7 us -> 0 us
  starting transfers between devices: 26.7 us -> 0 us
  other arithmetic: 22.3 us -> 0 us
    pallas_call x0 -> x1, Pallas kernels: none -> 55.2 us  [on_device(): pl.pallas_call(functools.partial(relay_kernel, sections, experts), out_sh...]
    gather x9 -> x0, local copies, waits for them, and re-layouts: 53.5 us -> none  [the longest x6 43.5 us: on_device(): picked_rows = jnp.take(flat_rows, flat_slot, axis=0)]
    all_to_all x6 -> x0, waiting for transfers between devices: 34.1 us -> none  [the longest x3 20.6 us: on_device(): lax.all_to_all(served.reshape(arrived_rows.shape), 'expert', split_axis=0...]
    ppermute x6 -> x0, waiting for transfers between devices: 30.2 us -> none  [shifted(): lax.ppermute(shard, axis, [(i, (i + by) % peers) for i in range(peers)])]
    dot_general x9 -> x0, matrix products: 26.7 us -> none  [the longest x3 11.9 us: expert_forward(): jnp.dot(token_rows, inner_weight, preferred_element_type=jnp.float32)]
    all_to_all x6 -> x0, starting transfers between devices: 26 us -> none  [the longest x3 13.4 us: on_device(): lax.all_to_all(outbound, 'expert', split_axis=0, concat_axis=0, tiled=True)]
    mul x10 -> x0, other arithmetic: 8.09 us -> none  [the longest x3 5.92 us: on_device(): jnp.take(normed, token_at, axis=0) * filled[:, :, None].astype(jnp.bfloat16)]
    reduce_sum x12 -> x0, other arithmetic: 5.68 us -> none  [the longest x3 4.17 us: normalize(): jnp.mean(widened * widened, axis=-1, keepdims=True) + epsilon]
  transfers between devices with their start and end apart: 12 -> 0, of which waited for: 9 -> 0; matrix products, arithmetic and copies ran while one was open for 36% -> 0% of each run, Pallas kernels for 0% -> 0%
where the time goes in v1:
time: 60.4 us; the launch traced here: 60.1 us
  Pallas kernels  55.2 us (91%)
  local copies, waits for them, and re-layouts  4.91 us (8%)
    pallas_call x1, Pallas kernels, on_device(): pl.pallas_call(functools.partial(relay_kernel, sections, experts), out_sh...  55.2 us
    unnamed x3, local copies, waits for them, and re-layouts  4.91 us

profile of v1, /device:TPU:0, one launch (start us, length us, event | category | flops | bytes accessed | tf_op | source)
XLA Modules:
  0.0 60.1 jit_solution(18260662905650057106)
XLA Ops:
  0.0 1.5 %copy.7.ids_ref = s32[3,1,128,6]{3,2,1,0:T(8,128)} copy(s32[3,1,128,6]{2,1,3,0:T(1,128)} %param.10) | data formatting | bytes 18432 | tf_op args[4]
  1.5 1.5 %copy.8.wts_ref = f32[3,1,128,6]{3,2,1,0:T(8,128)} copy(f32[3,1,128,6]{2,1,3,0:T(1,128)} %param.11) | data formatting | bytes 18432 | tf_op args[5]
  3.0 55.2 %relay.1 = bf16[1,128,2048]{2,1,0:T(8,128)(2,1)} custom-call(bf16[1,128,2048]{2,1,0:T(8,128)(2,1)} %state_ref.1, f32[1,2048]{1,0:T(1,128)} %gain_ref.1, bf16[1,1,2048,1536]{3,2,1,0:T(8,128)(2,1)} %win_hbm.1, bf16[1,1,768,2048]{3,2,1,0:T(8,128)(2,1)} %wout_hbm.1, s32[3,1,128,6]{3,2,1,0:T(8,128)} %copy.7.ids_ref, f32[3,1,128,6]{3,2,1,0:T(8,128)} %copy.8.wts_ref), custom_call_target="tpu_custom_call" | custom-call | tf_op jit(solution)/shard_map/relay/pallas_call | solution.py:266
  58.3 1.9 %copy.10 = bf16[1,128,2048]{2,1,0:T(8,128)(2,1)} copy(bf16[1,128,2048]{2,1,0:T(8,128)(2,1)} %relay.1) | data formatting | bytes 1048576

commit v2 on v1

v2 whole, which is shorter than its diff:
```python
import functools

import jax
import jax.numpy as jnp
from jax import lax
from jax.experimental import pallas as pl
from jax.experimental.pallas import tpu as pltpu
from jax.sharding import PartitionSpec as P

epsilon = 1e-06
CHUNKS = 4
PARTS = 2
LAG = 4
MESH = pl.DeviceIdType.MESH


def distances(experts):
    return list(range(1, experts))


def relay_kernel(
    sections,
    experts,
    state_ref,
    gain_ref,
    win_hbm,
    wout_hbm,
    ids_ref,
    wts_ref,
    out_ref,
    win,
    wout,
    hcur,
    hrecv,
    gather,
    comb_send,
    comb_recv,
    sendbuf,
    recvbuf,
    acc,
    retsend,
    retrecv,
    win_sem,
    wout_sem,
    disp_ss,
    disp_rs,
    ret_ss,
    ret_rs,
    h_ss,
    h_rs,
    comb_ss,
    comb_rs,
):
    ticks = ids_ref.shape[0]
    top = ids_ref.shape[1]
    tokens = state_ref.shape[1]
    width = state_ref.shape[2]
    chunks = win.shape[0]
    cols = width // chunks
    hidden_units = wout.shape[0]
    capacity = tokens // 4
    slots = experts * capacity
    parts = PARTS
    half = capacity // parts
    group = experts * half

    section = lax.axis_index("section")
    me = lax.axis_index("expert")
    after = lax.rem(section + 1, sections)
    before = lax.rem(section + sections - 1, sections)

    barrier = pltpu.get_barrier_semaphore()
    for d in range(1, experts):
        peer = lax.rem(me + d, experts)
        pl.semaphore_signal(
            barrier, inc=1, device_id={"section": section, "expert": peer}, device_id_type=MESH
        )
    for e in range(experts):
        for other in (after, before):
            pl.semaphore_signal(
                barrier, inc=1, device_id={"section": other, "expert": e}, device_id_type=MESH
            )

    def load_in(c):
        return pltpu.make_async_copy(
            win_hbm.at[0, 0, pl.ds(c * cols, cols)], win.at[c], win_sem.at[c]
        )

    load_out = pltpu.make_async_copy(wout_hbm.at[0, 0], wout, wout_sem)
    for c in range(chunks):
        load_in(c).start()
    load_out.start()

    slot_row = lax.broadcasted_iota(jnp.int32, (slots, tokens), 0)
    expert_of = jnp.zeros((slots, tokens), jnp.int32)
    slot_of = slot_row
    for p in range(parts):
        for e in range(experts):
            start = p * group + e * half
            inside = slot_row >= start
            expert_of = jnp.where(inside, e, expert_of)
            slot_of = jnp.where(inside, slot_row - start + p * half, slot_of)
    slot_of = slot_of.astype(jnp.float32)
    row_i = lax.broadcasted_iota(jnp.int32, (tokens, tokens), 0)
    col_i = lax.broadcasted_iota(jnp.int32, (tokens, tokens), 1)
    earlier = jnp.where(row_i < col_i, 1.0, 0.0).astype(jnp.bfloat16)

    def tables(t):
        hit = jnp.zeros((slots, tokens), jnp.float32)
        mix = jnp.zeros((slots, tokens), jnp.float32)
        for k in range(top):
            match = ids_ref[t, k] == expert_of
            hit = jnp.where(match, 1.0, hit)
            mix = jnp.where(match, wts_ref[t, k], mix)
        rank = jnp.dot(hit.astype(jnp.bfloat16), earlier, preferred_element_type=jnp.float32)
        keep = jnp.where(rank == slot_of, hit, 0.0)
        gather[t] = keep.astype(jnp.bfloat16)
        return keep * mix

    def comb_copy(t):
        return pltpu.make_async_remote_copy(
            src_ref=comb_send.at[t],
            dst_ref=comb_recv.at[t],
            send_sem=comb_ss.at[t],
            recv_sem=comb_rs.at[t],
            device_id={"section": after, "expert": me},
            device_id_type=MESH,
        )

    def send_comb(t, weighted):
        comb_send[t] = jnp.transpose(weighted).astype(jnp.bfloat16)
        comb_copy(t).start()

    def h_copy(t, c):
        source = state_ref.at[0, :, pl.ds(c * cols, cols)] if t == 0 else hcur.at[t - 1, c]
        return pltpu.make_async_remote_copy(
            src_ref=source,
            dst_ref=hrecv.at[t, c],
            send_sem=h_ss.at[t, c],
            recv_sem=h_rs.at[t, c],
            device_id={"section": after, "expert": me},
            device_id_type=MESH,
        )

    def send_rows(t, p, c):
        for d in distances(experts):
            peer = lax.rem(me + d, experts)
            pltpu.make_async_remote_copy(
                src_ref=sendbuf.at[t, c, pl.ds(p * group + peer * half, half)],
                dst_ref=recvbuf.at[t, c, pl.ds(p * group + me * half, half)],
                send_sem=disp_ss.at[t],
                recv_sem=disp_rs.at[t, p, c],
                device_id={"section": section, "expert": peer},
                device_id_type=MESH,
            ).start()

    def await_rows(t, p, c):
        block = recvbuf.at[t, c, pl.ds(p * group, group - half)]
        pltpu.make_async_remote_copy(
            src_ref=block,
            dst_ref=block,
            send_sem=disp_ss.at[t],
            recv_sem=disp_rs.at[t, p, c],
            device_id={"section": section, "expert": lax.rem(me + 1, experts)},
            device_id_type=MESH,
        ).wait_recv()

    def send_served(t, p, c):
        for d in distances(experts) + [0]:
            peer = lax.rem(me + d, experts)
            pltpu.make_async_remote_copy(
                src_ref=retsend.at[t, c, pl.ds(p * group + peer * half, half)],
                dst_ref=retrecv.at[t, c, pl.ds(p * group + me * half, half)],
                send_sem=ret_ss.at[t],
                recv_sem=ret_rs.at[t, c],
                device_id={"section": after, "expert": peer},
                device_id_type=MESH,
            ).start()

    def await_served(t, c):
        pltpu.make_async_remote_copy(
            src_ref=retrecv.at[t, c],
            dst_ref=retrecv.at[t, c],
            send_sem=ret_ss.at[t],
            recv_sem=ret_rs.at[t, c],
            device_id={"section": before, "expert": me},
            device_id_type=MESH,
        ).wait_recv()

    def fill(t, c, chunk):
        rows = jnp.dot(gather[t], chunk, preferred_element_type=jnp.float32)
        sendbuf[t, c] = rows.astype(jnp.bfloat16)

    def keep_own(t, c):
        for p in range(parts):
            own = pl.ds(pl.multiple_of(p * group + me * half, half), half)
            recvbuf[t, c, own, :] = sendbuf[t, c, own, :]

    def dispatch(t, c):
        send_rows(t, 0, c)
        for p in range(1, parts):
            late = c - p * LAG
            if late >= 0:
                send_rows(t, p, late)
        if c == chunks - 1:
            for p in range(1, parts):
                for late in range(max(chunks - p * LAG, 0), chunks):
                    send_rows(t, p, late)

    weighted = tables(0)
    for c in range(chunks):
        fill(0, c, state_ref[0, :, pl.ds(c * cols, cols)])
        if c == 0:
            pl.semaphore_wait(barrier, experts - 1 + 2 * experts)
        dispatch(0, c)
    for c in range(chunks):
        keep_own(0, c)
        h_copy(0, c).start()
    send_comb(0, weighted)
    for t in range(1, ticks):
        send_comb(t, tables(t))

    for t in range(ticks):
        for p in range(parts):
            rows = pl.ds(p * group, group)
            squares = jnp.zeros((group, 1), jnp.float32)
            for c in range(chunks):
                if t == 0 and p == 0:
                    load_in(c).wait()
                await_rows(t, p, c)
                wide = recvbuf[t, c, rows, :].astype(jnp.float32)
                squares = squares + jnp.sum(wide * wide, axis=-1, keepdims=True)
                scaled = (wide * gain_ref[:, pl.ds(c * cols, cols)]).astype(jnp.bfloat16)
                part = jnp.dot(scaled, win[c], preferred_element_type=jnp.float32)
                if c == 0:
                    acc[...] = part
                else:
                    acc[...] += part
            rescale = lax.rsqrt(squares / width + epsilon)
            gate = acc[:, :hidden_units] * rescale
            up = acc[:, hidden_units:] * rescale
            activated = (gate / (1.0 + jnp.exp(-gate)) * up).astype(jnp.bfloat16)
            if t == 0 and p == 0:
                load_out.wait()
            for c in range(chunks):
                served = jnp.dot(
                    activated, wout[:, pl.ds(c * cols, cols)], preferred_element_type=jnp.float32
                )
                retsend[t, c, rows, :] = served.astype(jnp.bfloat16)
                send_served(t, p, c)
        for c in range(chunks):
            if c == 0:
                comb_copy(t).wait_recv()
            h_copy(t, c).wait_recv()
            await_served(t, c)
            branch = jnp.dot(comb_recv[t], retrecv[t, c], preferred_element_type=jnp.float32)
            fresh = (hrecv[t, c].astype(jnp.float32) + branch).astype(jnp.bfloat16)
            if t == ticks - 1:
                out_ref[0, :, pl.ds(c * cols, cols)] = fresh
            else:
                hcur[t, c] = fresh
                fill(t + 1, c, fresh)
                dispatch(t + 1, c)
                h_copy(t + 1, c).start()
                keep_own(t + 1, c)

    for t in range(ticks):
        comb_copy(t).wait_send()
        for c in range(chunks):
            h_copy(t, c).wait_send()
        sent = sendbuf.at[t, :, pl.ds(0, slots - capacity)]
        pltpu.make_async_remote_copy(
            src_ref=sent,
            dst_ref=sent,
            send_sem=disp_ss.at[t],
            recv_sem=disp_rs.at[t, 0, 0],
            device_id={"section": after, "expert": me},
            device_id_type=MESH,
        ).wait_send()
        pltpu.make_async_remote_copy(
            src_ref=retsend.at[t],
            dst_ref=retrecv.at[t],
            send_sem=ret_ss.at[t],
            recv_sem=ret_rs.at[t, 0],
            device_id={"section": after, "expert": me},
            device_id_type=MESH,
        ).wait_send()


def on_device(sections, experts, state, norm_gain, expert_in, expert_out, route_ids, route_weights):
    ticks = route_ids.shape[0]
    tokens, width = state.shape[1:]
    inner = expert_in.shape[3]
    hidden_units = expert_out.shape[2]
    slots = experts * (tokens // 4)
    group = slots // PARTS
    cols = width // CHUNKS
    bf16 = jnp.bfloat16
    vmem = pl.BlockSpec(memory_space=pltpu.VMEM)
    hbm = pl.BlockSpec(memory_space=pl.ANY)
    dma = pltpu.SemaphoreType.DMA
    return pl.pallas_call(
        functools.partial(relay_kernel, sections, experts),
        out_shape=jax.ShapeDtypeStruct(state.shape, state.dtype),
        in_specs=[vmem, vmem, hbm, hbm, vmem, vmem],
        out_specs=vmem,
        scratch_shapes=[
            pltpu.VMEM((CHUNKS, cols, inner), bf16),
            pltpu.VMEM((hidden_units, width), bf16),
            pltpu.VMEM((max(ticks - 1, 1), CHUNKS, tokens, cols), bf16),
            pltpu.VMEM((ticks, CHUNKS, tokens, cols), bf16),
            pltpu.VMEM((ticks, slots, tokens), bf16),
            pltpu.VMEM((ticks, tokens, slots), bf16),
            pltpu.VMEM((ticks, tokens, slots), bf16),
            pltpu.VMEM((ticks, CHUNKS, slots, cols), bf16),
            pltpu.VMEM((ticks, CHUNKS, slots, cols), bf16),
            pltpu.VMEM((group, inner), jnp.float32),
            pltpu.VMEM((ticks, CHUNKS, slots, cols), bf16),
            pltpu.VMEM((ticks, CHUNKS, slots, cols), bf16),
            dma((CHUNKS,)),
            dma,
            dma((ticks,)),
            dma((ticks, PARTS, CHUNKS)),
            dma((ticks,)),
            dma((ticks, CHUNKS)),
            dma((ticks, CHUNKS)),
            dma((ticks, CHUNKS)),
            dma((ticks,)),
            dma((ticks,)),
        ],
        compiler_params=pltpu.CompilerParams(
            collective_id=0, has_side_effects=True, vmem_limit_bytes=60 * 1024 * 1024
        ),
        name="relay",
    )(
        state,
        norm_gain,
        expert_in,
        expert_out,
        jnp.transpose(route_ids, (0, 3, 1, 2)),
        jnp.transpose(route_weights, (0, 3, 1, 2)),
    )


def solution(mesh):
    in_specs = (
        P("section", "expert", None),
        P("section", None),
        P("section", "expert", None, None),
        P("section", "expert", None, None),
        P(None, "section", "expert", None),
        P(None, "section", "expert", None),
    )
    out_specs = P("section", "expert", None)
    return jax.shard_map(
        functools.partial(on_device, mesh.shape["section"], mesh.shape["expert"]),
        mesh=mesh,
        in_specs=in_specs,
        out_specs=out_specs,
        check_vma=False,
    )
```

time: 60.4 us -> 51.9 us (0.86)
  Pallas kernels: 55.2 us -> 49.8 us
  local copies, waits for them, and re-layouts: 4.91 us -> 1.88 us
    pallas_call x1, Pallas kernels: 55.2 us -> 49.8 us  [on_device(): pl.pallas_call(functools.partial(relay_kernel, sections, experts), out_sh...]
    unnamed x3 -> x1, local copies, waits for them, and re-layouts: 4.91 us -> 1.88 us
where the time goes in v2:
time: 51.9 us; the launch traced here: 51.7 us
  Pallas kernels  49.8 us (96%)
  local copies, waits for them, and re-layouts  1.88 us (4%)
    pallas_call x1, Pallas kernels, on_device(): pl.pallas_call(functools.partial(relay_kernel, sections, experts), out_sh...  49.8 us
    unnamed x1, local copies, waits for them, and re-layouts  1.88 us

profile of v2, /device:TPU:0, one launch (start us, length us, event | category | flops | bytes accessed | tf_op | source)
XLA Modules:
  0.0 51.7 jit_solution(4722913243699691109)
XLA Ops:
  0.0 49.8 %relay.1 = bf16[1,128,2048]{2,1,0:T(8,128)(2,1)} custom-call(bf16[1,128,2048]{2,1,0:T(8,128)(2,1)} %state_ref.1, f32[1,2048]{1,0:T(1,128)} %gain_ref.1, bf16[1,1,2048,1536]{3,2,1,0:T(8,128)(2,1)} %win_hbm.1, bf16[1,1,768,2048]{3,2,1,0:T(8,128)(2,1)} %wout_hbm.1, s32[3,6,1,128]{3,2,1,0:T(1,128)} %bitcast.2, f32[3,6,1,128]{3,2,1,0:T(1,128)} %bitcast.3), custom_call_target="tpu_custom_call" | custom-call | tf_op jit(solution)/shard_map/relay/pallas_call | solution.py:302
  49.8 1.9 %copy.8 = bf16[1,128,2048]{2,1,0:T(8,128)(2,1)} copy(bf16[1,128,2048]{2,1,0:T(8,128)(2,1)} %relay.1) | data formatting | bytes 1048576
